TPU v7x, 128 devices: a whole 4x4x4 slice. The times are simulated.
128 devices in a mesh: src: 8 (over x_lo, y), col: 16 (over x_hi, z, core).
Axes of the slice: x: 4 (x_hi: 2, x_lo: 2; x = x_hi * 2 + x_lo), y: 4, z: 4, core: 2. Of those that a mesh axis runs over, the one named last changes fastest.
Arguments:
- saved_tables: float32 [8, 65536, 256], P('src', 'col'), may hold values from -6 to 6
- saved_state: float32 [8, 65536], P('src', 'col'), may hold values from 0.05 to 4
- slot_table: int32 [8], replicated, may hold values from 0 to 7, each once
- row_ids: int32 [8, 2048], replicated, may hold values from 0 to 65535
- grads: float32 [8, 256, 2048], P('src', 'col'), may hold values from -6 to 6
Outputs:
- tables_out: float32 [8, 256, 65536], P('src', 'col')
- state_out: float32 [8, 65536], P('src')
Inputs may be any that keep to these rules, and one draw needn't show every extreme that they name: `slot_table`: each table is in exactly one slot. `row_ids`: row ids may repeat.
All inputs are finite; a program needn't handle non-finite values.
Results may differ from a plain program's by a relative error of at most 0.00002.
Values sent between devices are 32-bit elements; how exact they have to be, the bound alone decides.
A program may use at most 192 MiB of HBM per device.

v0:
```python
import functools

import jax
import jax.numpy as jnp
from jax import lax
from jax.sharding import Mesh
from jax.sharding import PartitionSpec as P

D = 256
COL = ("col_0", "col_1", "col_2")


learn_rate = 0.5
epsilon = 1e-08


def laid_out(blocks, dim):
    blocks = jnp.moveaxis(blocks, 0, dim)
    shape = blocks.shape
    return blocks.reshape(*shape[:dim], shape[dim] * shape[dim + 1], *shape[dim + 2 :])


def sent_to_all(array, axis):
    copies = jnp.broadcast_to(array, (lax.axis_size(axis), *array.shape))
    return lax.all_to_all(copies, axis, split_axis=0, concat_axis=0, tiled=True)


def gather_directly(array, axis, dim):
    return laid_out(sent_to_all(array, axis), dim)


def one_axis_at_a_time(array, axes):
    return functools.reduce(lax.psum, axes, array)


def reshard(tables, state):
    by_columns = lax.all_to_all(tables, COL, split_axis=2, concat_axis=1, tiled=True)
    state_full = gather_directly(state, COL, 1)
    return (by_columns, state_full)


def slot_inputs(slot_table, row_ids, every_grad):
    table = slot_table[lax.axis_index("src")]
    slot_ids = lax.dynamic_index_in_dim(row_ids, table, 0, keepdims=False)
    slot_grad = lax.dynamic_index_in_dim(every_grad, table, 0, keepdims=False)
    return (slot_ids, slot_grad)


def target_update(saved_tables, saved_state, slot_table, row_ids, grads):
    tables, state = reshard(saved_tables, saved_state)
    length = tables.shape[1]
    every_grad = gather_directly(grads, "src", 0)
    slot_ids, slot_grad = slot_inputs(slot_table, row_ids, every_grad)
    summed = jnp.zeros((length, slot_grad.shape[0]), jnp.float32).at[slot_ids].add(slot_grad.T)
    partial_value = jnp.sum(summed * summed, axis=1)
    picked = jnp.take(partial_value, slot_ids)
    used_total = one_axis_at_a_time(picked, COL)
    total = jnp.zeros((length,), jnp.float32).at[slot_ids].set(used_total)
    new_state = state[0] + total / D
    new_tables = tables[0] - learn_rate * summed / (jnp.sqrt(new_state)[:, None] + epsilon)
    return (new_tables.T[None], new_state[None])


def body(saved_tables, saved_state, slot_table, row_ids, grads):
    return target_update(saved_tables, saved_state, slot_table, row_ids, grads)


def solution(mesh):
    torus = Mesh(
        mesh.devices.reshape(mesh.shape["src"], 2, 4, 2), ("src", "col_0", "col_1", "col_2")
    )
    in_specs = (P("src", COL, None), P("src", COL), P(), P(), P("src", COL, None))
    out_specs = (P("src", COL, None), P("src", None))
    return jax.shard_map(body, mesh=torus, in_specs=in_specs, out_specs=out_specs, check_vma=False)
```

profile of v0, /device:TPU:1, one launch (start us, length us, event | category | flops | bytes accessed | tf_op | source)
XLA Modules:
  0.0 205.8 jit_solution(461164945287707107)
XLA Ops:
  0.6 0.9 broadcast_in_dim.29
  1.5 17.8 %all_to_all.25 = f32[16,1,4096]{2,1,0:T(1,128)S(1)} all-to-all(f32[16,1,4096]{2,1,0:T(1,128)S(1)} %broadcast_in_dim.29), channel_id=1, replica_groups=mesh['src'=8,'col_0'=2,'col_1'=4,'col_2'=2] {'col_0','col_1','col_2'}, dimensions={0} | all-to-all | bytes 524288 | tf_op jit(solution)/shard_map/all_to_all | solution.py:25
  19.3 2.0 broadcast_in_dim.28
  21.3 4.2 %all-to-all-start.1 = ((f32[8,1,16,2048]{3,2,1,0:T(8,128)}), f32[8,1,16,2048]{3,2,1,0:T(8,128)S(1)}, u32[]{:S(2)}, u32[]{:S(2)}) async-start(f32[8,1,16,2048]{3,2,1,0:T(8,128)} %broadcast_in_dim.28), calls=%async_computation.1 | async-start | bytes 2097152 | tf_op jit(solution)/shard_map/all_to_all | solution.py:25
  25.5 1.2 dynamic_slice.11
  28.1 10.1 %copy.17 = f32[1,4096,256]{1,0,2:T(1,128)} copy(f32[1,4096,256]{2,1,0:T(8,128)} %param.5) | data formatting | bytes 8388608 | tf_op args[0]
  38.9 1.6 all-to-all-done.1
  40.5 5.1 %all-to-all-start = ((f32[1,4096,256]{1,0,2:T(1,128)}), f32[1,4096,256]{1,0,2:T(1,128)}, u32[]{:S(2)}, u32[]{:S(2)}) async-start(f32[1,4096,256]{1,0,2:T(1,128)} %copy.17), calls=%async_computation | async-start | bytes 8388608 | tf_op jit(solution)/shard_map/all_to_all | solution.py:37
  45.6 0.9 compare_select_fusion
  46.4 0.3 copy.19
  46.8 24.6 %scatter_custom_fusion = f32[65536,16]{1,0:T(8,128)} fusion(s32[2048]{0:T(1024)S(1)} %bitcast.28, f32[2048,16]{1,0:T(8,128)S(1)} %copy.19, f32[]{:T(128)} %constant.16.clone.1), kind=kCustom, calls=%fused_computation.5 | custom fusion | flops 32768 | bytes 4194308 | tf_op jit(solution)/shard_map/scatter-add | solution.py:54
  71.4 15.3 %multiply_reduce_fusion = f32[65536]{0:T(1024)S(1)} fusion(f32[65536,16]{1,0:T(8,128)} %scatter_custom_fusion), kind=kLoop, calls=%fused_computation.4 | loop fusion | flops 2031616 | bytes 4456448 | tf_op jit(solution)/shard_map/reduce_sum | solution.py:55
  86.7 11.8 %gather_fusion = f32[2048]{0:T(1024)S(1)} fusion(f32[65536]{0:T(1024)S(1)} %multiply_reduce_fusion, s32[2048]{0:T(1024)S(1)} %broadcast_clamp_fusion), kind=kCustom, calls=%fused_computation | custom fusion | bytes 24576 | tf_op jit(solution)/shard_map/jit(_take)/gather | solution.py:56
  98.5 5.4 %psum.21 = f32[2048]{0:T(1024)S(1)} all-reduce(f32[2048]{0:T(1024)S(1)} %and_select_fusion), channel_id=1, replica_groups=mesh['src'=8,'col_0'=2,'col_1'=4,'col_2'=2] {'col_0'}, use_global_device_ids=true, to_apply=%region_2.3 | all-reduce | flops 2048 | bytes 16384 | tf_op jit(solution)/shard_map/psum | solution.py:33
  103.8 9.0 %psum.22 = f32[2048]{0:T(1024)S(1)} all-reduce(f32[2048]{0:T(1024)S(1)} %psum.21), channel_id=1, replica_groups=mesh['src'=8,'col_0'=2,'col_1'=4,'col_2'=2] {'col_1'}, use_global_device_ids=true, to_apply=%region_3.4 | all-reduce | flops 2048 | bytes 16384 | tf_op jit(solution)/shard_map/psum | solution.py:33
  112.8 5.4 %psum.23 = f32[2048]{0:T(1024)S(1)} all-reduce(f32[2048]{0:T(1024)S(1)} %psum.22), channel_id=1, replica_groups=mesh['src'=8,'col_0'=2,'col_1'=4,'col_2'=2] {'col_2'}, use_global_device_ids=true, to_apply=%region_4.5 | all-reduce | flops 2048 | bytes 16384 | tf_op jit(solution)/shard_map/psum | solution.py:33
  118.3 8.3 %scatter_custom_fusion.1 = f32[65536]{0:T(1024)S(1)} fusion(s32[2048]{0:T(1024)S(1)} %bitcast.29, f32[2048]{0:T(1024)S(1)} %psum.23, f32[]{:T(128)} %constant.16.clone.1), kind=kCustom, calls=%fused_computation.9 | custom fusion | bytes 262148 | tf_op jit(solution)/shard_map/scatter | solution.py:58
  126.6 0.8 sqrt_add_fusion
  127.4 0.0 all-to-all-done
  127.4 8.0 %copy.21 = f32[1,4096,256]{1,2,0:T(8,128)} copy(f32[1,4096,256]{1,0,2:T(1,128)} %all-to-all-done) | data formatting | bytes 8388608
  135.4 17.2 %copy.18 = f32[1,16,4096,16]{3,2,1,0:T(8,128)} copy(f32[1,16,4096,16]{2,3,1,0:T(8,128)} %bitcast.22) | data formatting | bytes 8388608 | tf_op jit(solution)/shard_map/all_to_all | solution.py:37
  152.5 34.2 %bitcast_subtract_fusion = f32[65536,16]{1,0:T(8,128)} fusion(f32[1,16,4096,16]{3,2,1,0:T(8,128)} %copy.18, f32[65536,16]{1,0:T(8,128)} %scatter_custom_fusion, f32[65536]{0:T(1024)S(1)} %get-tuple-element.10), kind=kLoop, calls=%fused_computation.3 | loop fusion | flops 3145728 | bytes 12845056 | tf_op jit(solution)/shard_map/sub | solution.py:60
  186.7 19.1 %copy.20 = f32[1,16,65536]{2,1,0:T(8,128)} copy(f32[1,16,65536]{1,2,0:T(8,128)} %bitcast.21) | data formatting | bytes 8388608
  (3 shorter events, 0.0 us)
Async XLA Ops:
  21.3 19.2 %all-to-all-start.1 = ((f32[8,1,16,2048]{3,2,1,0:T(8,128)}), f32[8,1,16,2048]{3,2,1,0:T(8,128)S(1)}, u32[]{:S(2)}, u32[]{:S(2)}) async-start(f32[8,1,16,2048]{3,2,1,0:T(8,128)} %broadcast_in_dim.28), calls=%async_computation.1 | async-start | bytes 2097152 | tf_op jit(solution)/shard_map/all_to_all | solution.py:25
  40.5 86.9 %all-to-all-start = ((f32[1,4096,256]{1,0,2:T(1,128)}), f32[1,4096,256]{1,0,2:T(1,128)}, u32[]{:S(2)}, u32[]{:S(2)}) async-start(f32[1,4096,256]{1,0,2:T(1,128)} %copy.17), calls=%async_computation | async-start | bytes 8388608 | tf_op jit(solution)/shard_map/all_to_all | solution.py:37
where the time goes:
time: 208 us; the launch traced here: 206 us
  local copies, waits for them, and re-layouts  78.9 us (38%)
  other arithmetic  75.7 us (36%)
  blocking collectives  37.5 us (18%)
  starting transfers between devices  9.27 us (4%)
  between operations  2.66 us (1%)
    unnamed x3, local copies, waits for them, and re-layouts  37.2 us
    sub x1, other arithmetic, target_update(): tables[0] - learn_rate * summed / (jnp.sqrt(new_state)[:, None] + epsilon)  34.2 us
    scatter-add x1, other arithmetic, target_update(): jnp.zeros((length, slot_grad.shape[0]), jnp.float32).at[slot_ids]  24.6 us
    psum x3, blocking collectives, one_axis_at_a_time(): return functools.reduce(lax.psum, axes, array)  19.8 us
    all_to_all x1, blocking collectives, sent_to_all(): return lax.all_to_all(copies, axis, split_axis=0, concat_axis=0, tiled=True)  17.8 us
    all_to_all x1, local copies, waits for them, and re-layouts, reshard(): lax.all_to_all(tables, COL, split_axis=2, concat_axis=1, tiled=True)  17.2 us
    reduce_sum x1, other arithmetic, target_update(): partial_value = jnp.sum(summed * summed, axis=1)  15.3 us
    gather x1, local copies, waits for them, and re-layouts, target_update(): picked = jnp.take(partial_value, slot_ids)  11.8 us
  transfers between devices with their start and end apart: 2, of which 1 were waited for; matrix products, arithmetic and copies ran while one was open for 36% of the time, Pallas kernels for 0%

commit v1 on v0

v1 whole, which is shorter than its diff:
```python
import jax
import jax.numpy as jnp
from jax import lax
from jax.experimental import pallas as pl
from jax.experimental.pallas import tpu as pltpu
from jax.sharding import Mesh
from jax.sharding import PartitionSpec as P

D = 256
ROWS = 65536
UPD = 2048
NT = 8
NC = 16
BLK = ROWS // NC
SRC = ("xl", "y")
COL = ("xh", "z", "c")
MESH = pl.DeviceIdType.MESH
f32, bf16 = jnp.float32, jnp.bfloat16

learn_rate = 0.5
epsilon = 1e-08

FIRST = [(1, 2, 0), (0, 2, 0), (0, 1, 0), (0, 3, 0)]
SECOND = [(1, 2, 1), (1, 1, 0), (0, 2, 1)]
THIRD = [(1, 3, 1), (1, 3, 0), (1, 1, 1), (1, 0, 0), (1, 0, 1), (0, 1, 1), (0, 3, 1), (0, 0, 1)]
PEERS = FIRST + SECOND + THIRD
OTHERS = [(1, 2), (0, 2), (1, 1), (1, 3), (1, 0), (0, 1), (0, 3)]
CHUNKS = 8


def kernel(tab, st, slot, ids_all, grads, out, state_out, tabv, tT, gv, rA, sB, rB, ids_t,
           hot, hot1, acc, summed, X, stf, qs, rq, rs, seml, ssem, rsem, sst, rst, sq, rq_sem, sA, rsA, sBs, rsB):
    xl, y, xh, z, c = (lax.axis_index(a) for a in SRC + COL)
    src = xl * 4 + y
    col = xh * 8 + z * 2 + c

    def peer(o):
        nxh, nz, nc = lax.rem(xh + o[0], 2), lax.rem(z + o[1], 4), lax.rem(c + o[2], 2)
        return (xl, y, nxh, nz, nc), nxh * 8 + nz * 2 + nc

    def source(o):
        nxh, nz, nc = lax.rem(xh + 2 - o[0], 2), lax.rem(z + 4 - o[1], 4), lax.rem(c + 2 - o[2], 2)
        return nxh * 8 + nz * 2 + nc

    def other(o):
        nxl, ny = lax.rem(xl + o[0], 2), lax.rem(y + o[1], 4)
        return (nxl, ny, xh, z, c), nxl * 4 + ny

    rows = BLK // CHUNKS
    loads = []
    gl = pltpu.make_async_copy(grads.at[0], gv, seml.at[CHUNKS])
    gl.start()
    sl = pltpu.make_async_copy(st, stf.at[pl.ds(pl.multiple_of(col * 32, 32), 32)], seml.at[CHUNKS + 1])
    sl.start()
    for i in range(CHUNKS):
        cp = pltpu.make_async_copy(tab.at[0, pl.ds(i * rows, rows)], tabv.at[pl.ds(i * rows, rows)], seml.at[i])
        cp.start()
        loads.append(cp)

    barrier = pltpu.get_barrier_semaphore()
    for o in PEERS:
        pl.semaphore_signal(barrier, inc=1, device_id=peer(o)[0], device_id_type=MESH)
    for o in OTHERS:
        pl.semaphore_signal(barrier, inc=1, device_id=other(o)[0], device_id_type=MESH)

    for i in range(CHUNKS):
        loads[i].wait()
        for h in range(2):
            part = tabv[pl.ds(i * rows, rows), pl.ds(h * 128, 128)]
            tT[pl.ds(h * 8, 8), :, pl.ds(i * rows, rows)] = part.T.reshape(8, 16, rows)
    gl.wait()
    sl.wait()
    pl.semaphore_wait(barrier, len(PEERS) + len(OTHERS))

    sends_a = []
    for i, o in enumerate(OTHERS):
        device, k = other(o)
        cp = pltpu.make_async_remote_copy(
            src_ref=gv.at[:, pl.ds(pl.multiple_of(k * 256, 256), 256)], dst_ref=rA.at[src],
            send_sem=sA.at[i], recv_sem=rsA.at[i], device_id=device, device_id_type=MESH)
        cp.start()
        sends_a.append(cp)
    sends_s, sends_t = [], {}
    for i, o in enumerate(PEERS):
        own = stf.at[pl.ds(pl.multiple_of(col * 32, 32), 32)]
        cp = pltpu.make_async_remote_copy(
            src_ref=own, dst_ref=own, send_sem=sst.at[i], recv_sem=rst.at[i],
            device_id=peer(o)[0], device_id_type=MESH)
        cp.start()
        sends_s.append(cp)

    def send_tables(group):
        for o in group:
            i = PEERS.index(o)
            device, k = peer(o)
            cp = pltpu.make_async_remote_copy(
                src_ref=tT.at[k], dst_ref=out.at[0, :, pl.ds(pl.multiple_of(col * BLK, BLK), BLK)],
                send_sem=ssem.at[i], recv_sem=rsem.at[i], device_id=device, device_id_type=MESH)
            cp.start()
            sends_t[o] = cp

    send_tables(FIRST)
    rA[src] = gv[:, pl.ds(pl.multiple_of(src * 256, 256), 256)]

    ids = ids_all[pl.ds(slot[src], 1), :]
    for i in range(16):
        tile = jnp.broadcast_to(ids[:, i * 128:(i + 1) * 128], (128, 128))
        ids_t[pl.ds(i * 128, 128), :] = tile.T
    lane = lax.broadcasted_iota(jnp.int32, (256, 128), 1)
    for i in range(8):
        at = jnp.bitwise_and(ids_t[pl.ds(i * 256, 256), :], 255)
        low = (at == lane).astype(f32)
        high = (at == lane + 128).astype(f32)
        hot[pl.ds(i * 256, 256), pl.ds(0, 128)] = low.astype(bf16)
        hot[pl.ds(i * 256, 256), pl.ds(128, 128)] = high.astype(bf16)
        hot1[pl.ds(i * 256, 256), :] = (low + high).astype(bf16)

    for cp in sends_a:
        cp.wait()
    sends_b = []
    for i, o in enumerate(OTHERS):
        device, k = other(o)
        sB[i] = rA[slot[k]]
    for i, o in enumerate(OTHERS):
        device, k = other(o)
        cp = pltpu.make_async_remote_copy(
            src_ref=sB.at[i], dst_ref=rB.at[src], send_sem=sBs.at[i], recv_sem=rsB.at[i],
            device_id=device, device_id_type=MESH)
        cp.start()
        sends_b.append(cp)
    send_tables(SECOND)
    rB[src] = rA[slot[src]]
    for cp in sends_b:
        cp.wait()

    def parts(v):
        a = v.astype(bf16)
        v = v - a.astype(f32)
        b = v.astype(bf16)
        v = v - b.astype(f32)
        return a, b, v.astype(bf16)

    g = [parts(rB[p]) for p in range(8)]
    g = [jnp.concatenate([g[p][k] for p in range(8)], axis=1) for k in range(3)]
    lhs = jnp.concatenate(g + [jnp.ones((16, UPD), bf16)], axis=0)

    for i in range(8):
        row = ids_t[pl.ds(i * 256, 256), :]
        same = jnp.concatenate(
            [(row == ids[:, k * 128:(k + 1) * 128]).astype(f32).astype(bf16) for k in range(16)], axis=1)
        part = jnp.dot(lhs[:, i * 256:(i + 1) * 256], same, preferred_element_type=f32)
        if i == 0:
            acc[...] = part
        else:
            acc[...] += part
    s = acc[0:16, :] + acc[16:32, :] + acc[32:48, :]
    count = acc[48:49, :]
    q = jnp.sum(s * s, axis=0, keepdims=True)
    qs[...] = q
    rq[col] = q
    sends_q = []
    for i, o in enumerate(PEERS):
        cp = pltpu.make_async_remote_copy(
            src_ref=qs, dst_ref=rq.at[col], send_sem=sq.at[i], recv_sem=rq_sem.at[i],
            device_id=peer(o)[0], device_id_type=MESH)
        cp.start()
        sends_q.append(cp)
    send_tables(THIRD)

    high = jnp.broadcast_to(lax.shift_right_logical(ids, 8).astype(f32).astype(bf16), (16, UPD))
    zero = jnp.zeros((16, UPD), bf16)

    def dense(it, _):
        for r in range(16):
            want = (it * 16 + r).astype(f32).astype(bf16)
            mask = high == want
            for k in range(3):
                X[pl.ds(k * 256 + r * 16, 16), :] = jnp.where(mask, g[k], zero)
        o = jnp.dot(X[...], hot[...], preferred_element_type=f32)
        o = o[0:256] + o[256:512] + o[512:768]
        for r in range(16):
            summed[:, pl.ds(pl.multiple_of((it * 16 + r) * 256, 256), 256)] = o[r * 16:(r + 1) * 16]
        return 0

    lax.fori_loop(0, 16, dense, 0)

    for cp in sends_s:
        cp.wait()
    for cp in sends_q:
        cp.wait()
    total = rq[0]
    for k in range(1, NC):
        total = total + rq[k]
    tp = [jnp.broadcast_to(t, (16, UPD)) for t in parts(total / count)]
    low = lax.shift_right_logical(ids, 7)
    for b in range(4):
        for r in range(8):
            row = lax.broadcasted_iota(jnp.int32, (16, UPD), 0) + (b * 128 + r * 16)
            mask = (row == jnp.broadcast_to(low, (16, UPD))).astype(f32).astype(bf16)
            for k in range(3):
                X[pl.ds(k * 128 + r * 16, 16), :] = mask * tp[k]
        o = jnp.dot(X[pl.ds(0, 384), :], hot1[...], preferred_element_type=f32)
        new = stf[pl.ds(b * 128, 128), :] + (o[0:128] + o[128:256] + o[256:384]) / D
        state_out[pl.ds(b * 128, 128), :] = new
        rs[pl.ds(b * 128, 128), :] = learn_rate / (jnp.sqrt(new) + epsilon)

    def update(k, landed):
        def tile(t, _):
            at = pl.multiple_of(k * BLK + t * 128, 128)
            scale = jnp.broadcast_to(rs[pl.ds(k * 32 + t, 1), :], (16, 128))
            v = out[0, :, pl.ds(at, 128)] if landed else tT[k, :, pl.ds(pl.multiple_of(t * 128, 128), 128)]
            out[0, :, pl.ds(at, 128)] = v - summed[:, pl.ds(at, 128)] * scale
            return 0
        lax.fori_loop(0, 32, tile, 0, unroll=8)

    update(col, False)
    for o in PEERS:
        sends_t[o].wait()
        update(source(o), True)


def body(saved_tables, saved_state, slot_table, row_ids, grads):
    n, m = len(PEERS), len(OTHERS)
    dma = pltpu.SemaphoreType.DMA
    vmem = pl.BlockSpec(memory_space=pltpu.VMEM)
    hbm = pl.BlockSpec(memory_space=pl.ANY)
    tables, state = pl.pallas_call(
        kernel,
        out_shape=(pltpu.VMEM((1, 16, ROWS), f32), pltpu.VMEM((512, 128), f32)),
        in_specs=[hbm, hbm, pl.BlockSpec(memory_space=pltpu.SMEM), vmem, hbm],
        out_specs=(vmem, vmem),
        scratch_shapes=[
            pltpu.VMEM((BLK, D), f32), pltpu.VMEM((NC, 16, BLK), f32), pltpu.VMEM((16, UPD), f32),
            pltpu.VMEM((8, 16, 256), f32), pltpu.VMEM((7, 16, 256), f32), pltpu.VMEM((8, 16, 256), f32),
            pltpu.VMEM((UPD, 128), jnp.int32), pltpu.VMEM((UPD, 256), bf16), pltpu.VMEM((UPD, 128), bf16),
            pltpu.VMEM((64, UPD), f32), pltpu.VMEM((16, ROWS), f32), pltpu.VMEM((768, UPD), bf16),
            pltpu.VMEM((512, 128), f32), pltpu.VMEM((1, UPD), f32), pltpu.VMEM((NC, 1, UPD), f32),
            pltpu.VMEM((512, 128), f32), dma((CHUNKS + 2,)), dma((n,)), dma((n,)), dma((n,)), dma((n,)),
            dma((n,)), dma((n,)), dma((m,)), dma((m,)), dma((m,)), dma((m,)),
        ],
        compiler_params=pltpu.CompilerParams(
            collective_id=0, has_side_effects=True, vmem_limit_bytes=48 << 20),
        name="restore",
    )(saved_tables, saved_state.reshape(32, 128), slot_table, row_ids, grads)
    return (tables, state.reshape(1, ROWS))


def solution(mesh):
    split = Mesh(mesh.devices.reshape(2, 4, 2, 4, 2), SRC + COL)
    in_specs = (P(SRC, COL, None), P(SRC, COL), P(), P(), P(SRC, COL, None))
    out_specs = (P(SRC, COL, None), P(SRC, None))
    return jax.shard_map(body, mesh=split, in_specs=in_specs, out_specs=out_specs, check_vma=False)
```

time: 208 us -> 70.3 us (0.34)
  other arithmetic: 75.7 us -> 0 us
  local copies, waits for them, and re-layouts: 78.9 us -> 5.83 us
  Pallas kernels: 0 us -> 63.6 us
  blocking collectives: 37.5 us -> 0 us
  starting transfers between devices: 9.27 us -> 0 us
    pallas_call x0 -> x1, Pallas kernels: none -> 63.6 us  [body(): pl.pallas_call(kernel, out_shape=(pltpu.VMEM((1, 16, ROWS), f32), pltpu.V...]
    sub x1 -> x0, other arithmetic: 34.2 us -> none  [target_update(): tables[0] - learn_rate * summed / (jnp.sqrt(new_state)[:, None] + epsilon)]
    unnamed x3 -> x10, local copies, waits for them, and re-layouts: 37.2 us -> 5.83 us
    scatter-add x1 -> x0, other arithmetic: 24.6 us -> none  [target_update(): jnp.zeros((length, slot_grad.shape[0]), jnp.float32).at[slot_ids]]
    psum x3 -> x0, blocking collectives: 19.8 us -> none  [one_axis_at_a_time(): return functools.reduce(lax.psum, axes, array)]
    all_to_all x1 -> x0, blocking collectives: 17.8 us -> none  [sent_to_all(): return lax.all_to_all(copies, axis, split_axis=0, concat_axis=0, tiled=True)]
    all_to_all x1 -> x0, local copies, waits for them, and re-layouts: 17.2 us -> none  [reshard(): lax.all_to_all(tables, COL, split_axis=2, concat_axis=1, tiled=True)]
    reduce_sum x1 -> x0, other arithmetic: 15.3 us -> none  [target_update(): partial_value = jnp.sum(summed * summed, axis=1)]
  transfers between devices with their start and end apart: 2 -> 0, of which waited for: 1 -> 0; matrix products, arithmetic and copies ran while one was open for 36% -> 0% of each run, Pallas kernels for 0% -> 0%
where the time goes in v1:
time: 70.3 us; the launch traced here: 70 us
  Pallas kernels  63.6 us (90%)
  local copies, waits for them, and re-layouts  5.83 us (8%)
    pallas_call x1, Pallas kernels, body(): pl.pallas_call(kernel, out_shape=(pltpu.VMEM((1, 16, ROWS), f32), pltpu.V...  63.6 us
    unnamed x10, local copies, waits for them, and re-layouts  5.83 us

profile of v1, /device:TPU:1, one launch (start us, length us, event | category | flops | bytes accessed | tf_op | source)
XLA Modules:
  0.0 70.0 jit_solution(14289428844113853329)
XLA Ops:
  0.6 0.0 copy-start
  0.6 0.9 %copy-done = f32[1,16,2048]{2,1,0:T(8,128)S(1)} copy-done((f32[1,16,2048]{2,1,0:T(8,128)S(1)}, f32[1,16,2048]{2,1,0:T(8,128)}, u32[]{:S(2)}) %copy-start) | copy-done | bytes 131096
  1.5 0.0 copy-start.1
  1.5 0.8 %copy-done.1 = s32[8,2048]{1,0:T(8,128)S(1)} copy-done((s32[8,2048]{1,0:T(8,128)S(1)}, s32[8,2048]{1,0:T(8,128)}, u32[]{:S(2)}) %copy-start.1) | copy-done | bytes 65560
  2.4 0.0 copy-start.2
  2.4 0.7 %copy-done.2 = f32[1,4096]{1,0:T(1,128)S(1)} copy-done((f32[1,4096]{1,0:T(1,128)S(1)}, f32[1,4096]{1,0:T(1,128)}, u32[]{:S(2)}) %copy-start.2) | copy-done | bytes 16408
  3.1 0.0 copy-start.3
  3.1 0.7 copy-done.3
  3.8 63.6 %restore.1 = (f32[1,16,65536]{2,1,0:T(8,128)S(1)}, f32[512,128]{1,0:T(8,128)S(1)}) custom-call(f32[1,4096,256]{2,1,0:T(8,128)} %tab.1, f32[32,128]{1,0:T(8,128)S(1)} %bitcast.3, s32[8]{0:T(128)S(1)} %copy-done.3, s32[8,2048]{1,0:T(8,128)S(1)} %copy-done.1, f32[1,16,2048]{2,1,0:T(8,128)S(1)} %copy-done), custom_call_target="tpu_custom_call" | custom-call | tf_op jit(solution)/shard_map/restore/pallas_call | solution.py:227
  67.3 2.0 %copy.9 = f32[1,16,65536]{2,1,0:T(8,128)} copy(f32[1,16,65536]{2,1,0:T(8,128)S(1)} %get-tuple-element.6) | data formatting | bytes 8388608
  69.3 0.7 %copy.10 = f32[1,65536]{1,0:T(1,128)} copy(f32[1,65536]{1,0:T(1,128)S(1)} %bitcast.2) | data formatting | bytes 524288
Async XLA Ops:
  0.6 0.9 %copy-start = (f32[1,16,2048]{2,1,0:T(8,128)S(1)}, f32[1,16,2048]{2,1,0:T(8,128)}, u32[]{:S(2)}) copy-start(f32[1,16,2048]{2,1,0:T(8,128)} %grads.1) | copy-start | bytes 393220
  1.5 0.8 %copy-start.1 = (s32[8,2048]{1,0:T(8,128)S(1)}, s32[8,2048]{1,0:T(8,128)}, u32[]{:S(2)}) copy-start(s32[8,2048]{1,0:T(8,128)} %ids_all.1) | copy-start | bytes 196612
  2.4 0.7 %copy-start.2 = (f32[1,4096]{1,0:T(1,128)S(1)}, f32[1,4096]{1,0:T(1,128)}, u32[]{:S(2)}) copy-start(f32[1,4096]{1,0:T(1,128)} %param.6) | copy-start | bytes 49156
  3.1 0.7 copy-start.3

commit v2 on v1

v2 whole, which is shorter than its diff:
```python
import jax
import jax.numpy as jnp
from jax import lax
from jax.experimental import pallas as pl
from jax.experimental.pallas import tpu as pltpu
from jax.sharding import Mesh
from jax.sharding import PartitionSpec as P

D = 256
ROWS = 65536
UPD = 2048
NT = 8
NC = 16
BLK = ROWS // NC
SRC = ("xl", "y")
COL = ("xh", "z", "c")
MESH = pl.DeviceIdType.MESH
f32, bf16 = jnp.float32, jnp.bfloat16

learn_rate = 0.5
epsilon = 1e-08

FIRST_X = [(1, 2, 0)]
FIRST_Z = [(0, 2, 0), (0, 1, 0), (0, 3, 0)]
SECOND = [(1, 2, 1), (1, 1, 0), (1, 3, 1)]
THIRD = [(0, 2, 1), (1, 0, 0), (1, 3, 0), (0, 1, 1), (0, 3, 1), (1, 1, 1), (1, 0, 1), (0, 0, 1)]
PEERS = FIRST_X + FIRST_Z + SECOND + THIRD
EARLY = FIRST_X + FIRST_Z + [(0, 0, 1)] + SECOND + [(0, 2, 1), (0, 1, 1), (0, 3, 1)]
LATE = [(1, 0, 0), (1, 3, 0), (1, 1, 1), (1, 0, 1)]
CHIPS = [(1, 2), (0, 2), (1, 1), (1, 3), (1, 0), (0, 1), (0, 3)]
OTHERS = [(1, 2), (0, 2), (1, 1), (1, 3), (1, 0), (0, 1), (0, 3)]
CHUNKS = 4


def source(o):
    xh, z, c = (lax.axis_index(a) for a in COL)
    xh, z, c = lax.rem(xh + 2 - o[0], 2), lax.rem(z + 4 - o[1], 4), lax.rem(c + 2 - o[2], 2)
    return xh * 8 + z * 2 + c


def update(k, out, summed, rs, read):
    def tile(t, _):
        at = pl.multiple_of(k * BLK + t * 128, 128)
        scale = jnp.broadcast_to(rs[pl.ds(k * 32 + t, 1), :], (16, 128))
        out[0, :, pl.ds(at, 128)] = read(at, t) - summed[:, pl.ds(at, 128)] * scale
        return 0
    lax.fori_loop(0, 32, tile, 0, unroll=8)


def kernel(tab, st, slot_h, ids_h, grads, out, state_out, summed, rs, slot, ids_all, tabv, tT, gv, rA, sB, rB,
           ids_t, hot, hot1, same, acc, X, stf, qs, qp, qh, rq, tot, seml, ssem, rsem, sst, rst, sq, rq_sem,
           sA, rsA, sBs, rsB):
    xl, y, xh, z, c = (lax.axis_index(a) for a in SRC + COL)
    src = xl * 4 + y
    col = xh * 8 + z * 2 + c

    def remote(a, b, sems, i, device):
        cp = pltpu.make_async_remote_copy(
            src_ref=a, dst_ref=b, send_sem=sems[0].at[i], recv_sem=sems[1].at[i],
            device_id=device, device_id_type=MESH)
        cp.start()
        return cp

    def peer(o):
        return (xl, y, lax.rem(xh + o[0], 2), lax.rem(z + o[1], 4), lax.rem(c + o[2], 2))

    def other(o):
        nxl, ny = lax.rem(xl + o[0], 2), lax.rem(y + o[1], 4)
        return (nxl, ny, xh, z, c), nxl * 4 + ny

    partner = peer((0, 0, 1))

    rows = BLK // CHUNKS
    first = pl.multiple_of((1 - xh) * 128, 128)
    second = pl.multiple_of(xh * 128, 128)
    small = []
    for i, (a, b) in enumerate([(grads.at[0], gv), (slot_h, slot), (ids_h, ids_all), (st, stf.at[xh, z, c])]):
        cp = pltpu.make_async_copy(a, b, seml.at[i])
        cp.start()
        small.append(cp)
    loads = []
    for h, lanes in enumerate((first, second)):
        for i in range(CHUNKS):
            cp = pltpu.make_async_copy(
                tab.at[0, pl.ds(i * rows, rows), pl.ds(lanes, 128)], tabv.at[h, pl.ds(i * rows, rows)],
                seml.at[4 + h * CHUNKS + i])
            cp.start()
            loads.append(cp)

    barrier = pltpu.get_barrier_semaphore()
    for o in PEERS:
        pl.semaphore_signal(barrier, inc=1, device_id=peer(o), device_id_type=MESH)
    for o in OTHERS:
        pl.semaphore_signal(barrier, inc=1, device_id=other(o)[0], device_id_type=MESH)

    def columns(h):
        for i in range(CHUNKS):
            loads[h * CHUNKS + i].wait()
            part = tabv[h, pl.ds(i * rows, rows), :]
            tT[h, :, :, pl.ds(i * rows, rows)] = part.T.reshape(8, 16, rows)

    sends_t = {}

    def send_tables(group):
        for o in group:
            nz, nc = lax.rem(z + o[1], 4), lax.rem(c + o[2], 2)
            sends_t[o] = remote(
                tT.at[1 - o[0], nz * 2 + nc], out.at[0, :, pl.ds(pl.multiple_of(col * BLK, BLK), BLK)],
                (ssem, rsem), PEERS.index(o), peer(o))

    columns(0)
    for cp in small:
        cp.wait()
    pl.semaphore_wait(barrier, len(PEERS) + len(OTHERS))

    sends_a = []
    for i, o in enumerate(OTHERS):
        device, k = other(o)
        sends_a.append(remote(gv.at[:, pl.ds(pl.multiple_of(k * 256, 256), 256)], rA.at[src], (sA, rsA), i, device))
    state_x = remote(stf.at[xh, z, c], stf.at[xh, z, c], (sst, rst), 0, peer((1, 0, 0)))
    send_tables(FIRST_X)
    columns(1)
    send_tables(FIRST_Z)
    rA[src] = gv[:, pl.ds(pl.multiple_of(src * 256, 256), 256)]

    ids = ids_all[pl.ds(slot[src], 1), :]
    for i in range(16):
        tile = jnp.broadcast_to(ids[:, i * 128:(i + 1) * 128], (128, 128))
        ids_t[pl.ds(i * 128, 128), :] = tile.T

    for cp in sends_a:
        cp.wait_recv()
    for i, o in enumerate(OTHERS):
        sB[i] = rA[slot[other(o)[1]]]
    rB[src] = rA[slot[src]]
    state_x.wait_recv()
    state_z = [remote(stf.at[:, z, c], stf.at[:, z, c], (sst, rst), i, peer((0, i, 0))) for i in (1, 2, 3)]
    sends_b = []
    for i, o in enumerate(OTHERS):
        sends_b.append(remote(sB.at[i], rB.at[src], (sBs, rsB), i, other(o)[0]))
    send_tables(SECOND)

    lane = lax.broadcasted_iota(jnp.int32, (256, 128), 1)
    for i in range(8):
        at = jnp.bitwise_and(ids_t[pl.ds(i * 256, 256), :], 255)
        low = (at == lane).astype(f32)
        high = (at == lane + 128).astype(f32)
        hot[pl.ds(i * 256, 256), pl.ds(0, 128)] = low.astype(bf16)
        hot[pl.ds(i * 256, 256), pl.ds(128, 128)] = high.astype(bf16)
        hot1[pl.ds(i * 256, 256), :] = (low + high).astype(bf16)
    for i in range(8):
        row = ids_t[pl.ds(i * 256, 256), :]
        for k in range(16):
            same[pl.ds(i * 256, 256), pl.ds(k * 128, 128)] = (
                row == ids[:, k * 128:(k + 1) * 128]).astype(f32).astype(bf16)

    def parts(v):
        a = v.astype(bf16)
        v = v - a.astype(f32)
        b = v.astype(bf16)
        v = v - b.astype(f32)
        return a, b, v.astype(bf16)

    for cp in sends_b:
        cp.wait_recv()
    g = [parts(rB[p]) for p in range(8)]
    g = [jnp.concatenate([g[p][k] for p in range(8)], axis=1) for k in range(3)]
    lhs = jnp.concatenate(g + [jnp.ones((16, UPD), bf16)], axis=0)

    for i in range(8):
        part = jnp.dot(lhs[:, i * 256:(i + 1) * 256], same[pl.ds(i * 256, 256), :], preferred_element_type=f32)
        if i == 0:
            acc[...] = part
        else:
            acc[...] += part
    s = acc[0:16, :] + acc[16:32, :] + acc[32:48, :]
    q = jnp.sum(s * s, axis=0, keepdims=True)
    qs[0] = q[:, :1024]
    qs[1] = q[:, 1024:]

    high = jnp.broadcast_to(lax.shift_right_logical(ids, 8).astype(f32).astype(bf16), (16, UPD))
    zero = jnp.zeros((16, UPD), bf16)

    def dense(it, _):
        for r in range(16):
            want = (it * 16 + r).astype(f32).astype(bf16)
            mask = high == want
            for k in range(3):
                X[pl.ds(k * 256 + r * 16, 16), :] = jnp.where(mask, g[k], zero)
        o = jnp.dot(X[...], hot[...], preferred_element_type=f32)
        o = o[0:256] + o[256:512] + o[512:768]
        for r in range(16):
            summed[:, pl.ds(pl.multiple_of((it * 16 + r) * 256, 256), 256)] = o[r * 16:(r + 1) * 16]
        return 0

    q_core = remote(qs.at[1 - c], qp, (sq, rq_sem), 7, partner)
    lax.fori_loop(0, 2, dense, 0)
    q_core.wait()
    half = qs[c] + qp[...]
    qh[...] = half
    rq[xh * 4 + z] = half
    lax.fori_loop(2, 3, dense, 0)
    sends_q = [remote(qh, rq.at[xh * 4 + z], (sq, rq_sem), i, peer((*o, 0))) for i, o in enumerate(CHIPS)]
    send_tables(THIRD)
    lax.fori_loop(3, 14, dense, 0)
    for cp in state_z:
        cp.wait_recv()
    state_c = remote(stf.at[:, :, c], stf.at[:, :, c], (sst, rst), 4, partner)
    for cp in sends_q:
        cp.wait_recv()
    total = rq[0]
    for k in range(1, 8):
        total = total + rq[k]
    tot[c] = total
    lax.fori_loop(14, 15, dense, 0)
    q_back = remote(tot.at[c], tot.at[c], (sq, rq_sem), 8, partner)
    lax.fori_loop(15, 16, dense, 0)
    q_back.wait_recv()
    state_c.wait_recv()

    total = jnp.concatenate([tot[0], tot[1]], axis=1) / acc[48:49, :]
    tp = [jnp.broadcast_to(t, (16, UPD)) for t in parts(total)]
    low = lax.shift_right_logical(ids, 7)
    for b in range(4):
        for r in range(8):
            row = lax.broadcasted_iota(jnp.int32, (16, UPD), 0) + (b * 128 + r * 16)
            mask = (row == jnp.broadcast_to(low, (16, UPD))).astype(f32).astype(bf16)
            for k in range(3):
                X[pl.ds(k * 128 + r * 16, 16), :] = mask * tp[k]
        o = jnp.dot(X[pl.ds(0, 384), :], hot1[...], preferred_element_type=f32)
        saved = stf[b // 2, (b % 2) * 2:(b % 2) * 2 + 2].reshape(128, 128)
        new = saved + (o[0:128] + o[128:256] + o[256:384]) / D
        state_out[pl.ds(b * 128, 128), :] = new
        rs[pl.ds(b * 128, 128), :] = learn_rate / (jnp.sqrt(new) + epsilon)

    update(col, out, summed, rs, lambda at, t: tT[1, z * 2 + c, :, pl.ds(pl.multiple_of(t * 128, 128), 128)])
    for o in EARLY:
        sends_t[o].wait_recv()
        update(source(o), out, summed, rs, lambda at, t: out[0, :, pl.ds(at, 128)])
    for o in LATE:
        sends_t[o].wait_recv()
    for cp in sends_a + sends_b + state_z + sends_q + [state_x, state_c, q_back]:
        cp.wait_send()
    for o in PEERS:
        sends_t[o].wait_send()


def finish(landed, state, summed, rs, out, state_out, sem):
    col = source((0, 0, 0))
    copies = [pltpu.make_async_copy(state, state_out, sem.at[16])]
    copies[0].start()

    def put(k):
        at = pl.ds(pl.multiple_of(k * BLK, BLK), BLK)
        cp = pltpu.make_async_copy(landed.at[0, :, at], out.at[0, :, at], sem.at[len(copies) - 1])
        cp.start()
        copies.append(cp)

    put(col)
    for o in EARLY:
        put(source(o))
    for o in LATE:
        update(source(o), landed, summed, rs, lambda at, t: landed[0, :, pl.ds(at, 128)])
        put(source(o))
    for cp in copies:
        cp.wait()


def body(saved_tables, saved_state, slot_table, row_ids, grads):
    n, m = len(PEERS), len(OTHERS)
    dma = pltpu.SemaphoreType.DMA
    vmem = pl.BlockSpec(memory_space=pltpu.VMEM)
    hbm = pl.BlockSpec(memory_space=pltpu.HBM)
    tables, state, summed, rs = pl.pallas_call(
        kernel,
        out_shape=(pltpu.VMEM((1, 16, ROWS), f32), pltpu.VMEM((512, 128), f32), pltpu.VMEM((16, ROWS), f32),
                   pltpu.VMEM((512, 128), f32)),
        in_specs=[hbm] * 5,
        out_specs=(vmem,) * 4,
        scratch_shapes=[
            pltpu.SMEM((8,), jnp.int32), pltpu.VMEM((8, UPD), jnp.int32),
            pltpu.VMEM((2, BLK, 128), f32), pltpu.VMEM((2, 8, 16, BLK), f32), pltpu.VMEM((16, UPD), f32),
            pltpu.VMEM((8, 16, 256), f32), pltpu.VMEM((7, 16, 256), f32), pltpu.VMEM((8, 16, 256), f32),
            pltpu.VMEM((UPD, 128), jnp.int32), pltpu.VMEM((UPD, 256), bf16), pltpu.VMEM((UPD, 128), bf16),
            pltpu.VMEM((UPD, UPD), bf16), pltpu.VMEM((64, UPD), f32), pltpu.VMEM((768, UPD), bf16),
            pltpu.VMEM((2, 4, 2, 32, 128), f32), pltpu.VMEM((2, 1, 1024), f32), pltpu.VMEM((1, 1024), f32),
            pltpu.VMEM((1, 1024), f32), pltpu.VMEM((8, 1, 1024), f32), pltpu.VMEM((2, 1, 1024), f32),
            dma((4 + 2 * CHUNKS,)), dma((n,)), dma((n,)), dma((5,)), dma((5,)),
            dma((9,)), dma((9,)), dma((m,)), dma((m,)), dma((m,)), dma((m,)),
        ],
        compiler_params=pltpu.CompilerParams(
            collective_id=0, has_side_effects=True, vmem_limit_bytes=44 << 20),
        name="restore",
    )(*(pltpu.with_memory_space_constraint(a, pltpu.HBM) for a in (
        saved_tables, saved_state.reshape(32, 128), slot_table, row_ids, grads)))
    tables, state = pl.pallas_call(
        finish,
        out_shape=(jax.ShapeDtypeStruct((1, 16, ROWS), f32), jax.ShapeDtypeStruct((512, 128), f32)),
        in_specs=[vmem] * 4,
        out_specs=(hbm, hbm),
        scratch_shapes=[dma((17,))],
        compiler_params=pltpu.CompilerParams(vmem_limit_bytes=16 << 20),
        name="finish",
    )(tables, state, summed, rs)
    return (tables, state.reshape(1, ROWS))


def solution(mesh):
    split = Mesh(mesh.devices.reshape(2, 4, 2, 4, 2), SRC + COL)
    in_specs = (P(SRC, COL, None), P(SRC, COL), P(), P(), P(SRC, COL, None))
    out_specs = (P(SRC, COL, None), P(SRC, None))
    return jax.shard_map(body, mesh=split, in_specs=in_specs, out_specs=out_specs, check_vma=False)
```

time: 70.3 us -> 62.3 us (0.89)
  local copies, waits for them, and re-layouts: 5.83 us -> 0 us
  Pallas kernels: 63.6 us -> 61.6 us
    unnamed x10 -> x0, local copies, waits for them, and re-layouts: 5.83 us -> none
    pallas_call x1, Pallas kernels: 63.6 us -> 59.3 us  [body(): pl.pallas_call(kernel, out_shape=(pltpu.VMEM((1, 16, ROWS), f32), pltpu.V...]
    pallas_call x0 -> x1, Pallas kernels: none -> 2.23 us  [body(): pl.pallas_call(finish, out_shape=(jax.ShapeDtypeStruct((1, 16, ROWS), f32...]
where the time goes in v2:
time: 62.3 us; the launch traced here: 62.2 us
  Pallas kernels  61.6 us (99%)
  between operations  0.64 us (1%)
    pallas_call x1, Pallas kernels, body(): pl.pallas_call(kernel, out_shape=(pltpu.VMEM((1, 16, ROWS), f32), pltpu.V...  59.3 us
    pallas_call x1, Pallas kernels, body(): pl.pallas_call(finish, out_shape=(jax.ShapeDtypeStruct((1, 16, ROWS), f32...  2.23 us

profile of v2, /device:TPU:1, one launch (start us, length us, event | category | flops | bytes accessed | tf_op | source)
XLA Modules:
  0.0 62.2 jit_solution(7113260310060923211)
XLA Ops:
  0.6 59.3 %restore.1 = (f32[1,16,65536]{2,1,0:T(8,128)S(1)}, f32[512,128]{1,0:T(8,128)S(1)}, f32[16,65536]{1,0:T(8,128)S(1)}, f32[512,128]{1,0:T(8,128)S(1)}) custom-call(f32[1,4096,256]{2,1,0:T(8,128)} %tab.1, f32[32,128]{1,0:T(8,128)} %bitcast.2, s32[8]{0:T(128)} %slot_h.1, s32[8,2048]{1,0:T(8,128)} %ids_h.1, f32[1,16,2048]{2,1,0:T(8,128)} %grads.1), custom_call_target="tpu_custom_call" | custom-call | tf_op jit(solution)/shard_map/restore/pallas_call | solution.py:274
  60.0 2.2 %finish.1 = (f32[1,16,65536]{2,1,0:T(8,128)}, f32[512,128]{1,0:T(8,128)}) custom-call(f32[1,16,65536]{2,1,0:T(8,128)S(1)} %get-tuple-element.8.landed, f32[512,128]{1,0:T(8,128)S(1)} %get-tuple-element.9.state, f32[16,65536]{1,0:T(8,128)S(1)} %get-tuple-element.10.summed, f32[512,128]{1,0:T(8,128)S(1)} %get-tuple-element.11.rs), custom_call_target="tpu_custom_call" | custom-call | tf_op jit(solution)/shard_map/finish/pallas_call | solution.py:296

commit v3 on v2

--- a/solution.py
+++ b/solution.py
@@ -20,22 +20,26 @@
 learn_rate = 0.5
 epsilon = 1e-08
 
-FIRST_X = [(1, 2, 0)]
-FIRST_Z = [(0, 2, 0), (0, 1, 0), (0, 3, 0)]
-SECOND = [(1, 2, 1), (1, 1, 0), (1, 3, 1)]
-THIRD = [(0, 2, 1), (1, 0, 0), (1, 3, 0), (0, 1, 1), (0, 3, 1), (1, 1, 1), (1, 0, 1), (0, 0, 1)]
+FIRST_X = [(1, 1, 0)]
+FIRST_Z = [(0, 1, 0), (0, 3, 0), (0, 2, 0)]
+SECOND = [(1, 2, 0), (1, 3, 0), (1, 0, 0)]
+THIRD = [(0, 1, 1), (1, 1, 1), (1, 2, 1), (0, 3, 1), (0, 2, 1), (1, 3, 1), (1, 0, 1), (0, 0, 1)]
 PEERS = FIRST_X + FIRST_Z + SECOND + THIRD
-EARLY = FIRST_X + FIRST_Z + [(0, 0, 1)] + SECOND + [(0, 2, 1), (0, 1, 1), (0, 3, 1)]
-LATE = [(1, 0, 0), (1, 3, 0), (1, 1, 1), (1, 0, 1)]
+EARLY = [(1, 1, 0), (0, 2, 0), (0, 1, 0), (0, 3, 0), (0, 0, 1), (1, 2, 0), (1, 0, 0), (1, 3, 0), (0, 2, 1), (0, 1, 1), (0, 3, 1)]
+LATE = [(1, 1, 1), (1, 2, 1), (1, 3, 1), (1, 0, 1)]
 CHIPS = [(1, 2), (0, 2), (1, 1), (1, 3), (1, 0), (0, 1), (0, 3)]
 OTHERS = [(1, 2), (0, 2), (1, 1), (1, 3), (1, 0), (0, 1), (0, 3)]
 CHUNKS = 4
 
 
+def turn(o, c):
+    return o[1] + 2 * c if o[0] else o[1]
+
+
 def source(o):
     xh, z, c = (lax.axis_index(a) for a in COL)
-    xh, z, c = lax.rem(xh + 2 - o[0], 2), lax.rem(z + 4 - o[1], 4), lax.rem(c + 2 - o[2], 2)
-    return xh * 8 + z * 2 + c
+    xh, c = lax.rem(xh + 2 - o[0], 2), lax.rem(c + 2 - o[2], 2)
+    return xh * 8 + lax.rem(z + 8 - turn(o, c), 4) * 2 + c
 
 
 def update(k, out, summed, rs, read):
@@ -69,6 +73,12 @@
         return (nxl, ny, xh, z, c), nxl * 4 + ny
 
     partner = peer((0, 0, 1))
+
+    barrier = pltpu.get_barrier_semaphore()
+    for o in PEERS:
+        pl.semaphore_signal(barrier, inc=1, device_id=peer(o), device_id_type=MESH)
+    for o in OTHERS:
+        pl.semaphore_signal(barrier, inc=1, device_id=other(o)[0], device_id_type=MESH)
 
     rows = BLK // CHUNKS
     first = pl.multiple_of((1 - xh) * 128, 128)
@@ -87,12 +97,6 @@
             cp.start()
             loads.append(cp)
 
-    barrier = pltpu.get_barrier_semaphore()
-    for o in PEERS:
-        pl.semaphore_signal(barrier, inc=1, device_id=peer(o), device_id_type=MESH)
-    for o in OTHERS:
-        pl.semaphore_signal(barrier, inc=1, device_id=other(o)[0], device_id_type=MESH)
-
     def columns(h):
         for i in range(CHUNKS):
             loads[h * CHUNKS + i].wait()
@@ -103,10 +107,10 @@
 
     def send_tables(group):
         for o in group:
-            nz, nc = lax.rem(z + o[1], 4), lax.rem(c + o[2], 2)
+            nz, nc = lax.rem(z + turn(o, c), 4), lax.rem(c + o[2], 2)
             sends_t[o] = remote(
                 tT.at[1 - o[0], nz * 2 + nc], out.at[0, :, pl.ds(pl.multiple_of(col * BLK, BLK), BLK)],
-                (ssem, rsem), PEERS.index(o), peer(o))
+                (ssem, rsem), PEERS.index(o), (xl, y, lax.rem(xh + o[0], 2), nz, nc))
 
     columns(0)
     for cp in small:

time: 62.3 us -> 62.2 us (level)
  Pallas kernels: 61.6 us -> 60.9 us
    pallas_call x1, Pallas kernels: 59.3 us -> 58.7 us  [body(): pl.pallas_call(kernel, out_shape=(pltpu.VMEM((1, 16, ROWS), f32), pltpu.V...]
where the time goes in v3:
time: 62.2 us; the launch traced here: 61.6 us
  Pallas kernels  60.9 us (98%)
  between operations  0.64 us (1%)
    pallas_call x1, Pallas kernels, body(): pl.pallas_call(kernel, out_shape=(pltpu.VMEM((1, 16, ROWS), f32), pltpu.V...  58.7 us
    pallas_call x1, Pallas kernels, body(): pl.pallas_call(finish, out_shape=(jax.ShapeDtypeStruct((1, 16, ROWS), f32...  2.23 us

profile of v3, /device:TPU:1, one launch (start us, length us, event | category | flops | bytes accessed | tf_op | source)
XLA Modules:
  0.0 61.6 jit_solution(18323351823539969714)
XLA Ops:
  0.6 58.7 %restore.1 = (f32[1,16,65536]{2,1,0:T(8,128)S(1)}, f32[512,128]{1,0:T(8,128)S(1)}, f32[16,65536]{1,0:T(8,128)S(1)}, f32[512,128]{1,0:T(8,128)S(1)}) custom-call(f32[1,4096,256]{2,1,0:T(8,128)} %tab.1, f32[32,128]{1,0:T(8,128)} %bitcast.2, s32[8]{0:T(128)} %slot_h.1, s32[8,2048]{1,0:T(8,128)} %ids_h.1, f32[1,16,2048]{2,1,0:T(8,128)} %grads.1), custom_call_target="tpu_custom_call" | custom-call | tf_op jit(solution)/shard_map/restore/pallas_call | solution.py:278
  59.3 2.2 %finish.1 = (f32[1,16,65536]{2,1,0:T(8,128)}, f32[512,128]{1,0:T(8,128)}) custom-call(f32[1,16,65536]{2,1,0:T(8,128)S(1)} %get-tuple-element.8.landed, f32[512,128]{1,0:T(8,128)S(1)} %get-tuple-element.9.state, f32[16,65536]{1,0:T(8,128)S(1)} %get-tuple-element.10.summed, f32[512,128]{1,0:T(8,128)S(1)} %get-tuple-element.11.rs), custom_call_target="tpu_custom_call" | custom-call | tf_op jit(solution)/shard_map/finish/pallas_call | solution.py:300

commit v4 on v3

--- a/solution.py
+++ b/solution.py
@@ -33,7 +33,7 @@
 
 
 def turn(o, c):
-    return o[1] + 2 * c if o[0] else o[1]
+    return o[1] + 3 * c if o[0] else o[1]
 
 
 def source(o):

time: 62.2 us -> 62.1 us (level)
  no operation moved by 1% of the time
where the time goes in v4:
time: 62.1 us; the launch traced here: 62 us
  Pallas kernels  61.3 us (99%)
  between operations  0.64 us (1%)
    pallas_call x1, Pallas kernels, body(): pl.pallas_call(kernel, out_shape=(pltpu.VMEM((1, 16, ROWS), f32), pltpu.V...  59.1 us
    pallas_call x1, Pallas kernels, body(): pl.pallas_call(finish, out_shape=(jax.ShapeDtypeStruct((1, 16, ROWS), f32...  2.23 us

profile of v4, /device:TPU:1, one launch (start us, length us, event | category | flops | bytes accessed | tf_op | source)
XLA Modules:
  0.0 62.0 jit_solution(2291961707294993164)
XLA Ops:
  0.6 59.1 %restore.1 = (f32[1,16,65536]{2,1,0:T(8,128)S(1)}, f32[512,128]{1,0:T(8,128)S(1)}, f32[16,65536]{1,0:T(8,128)S(1)}, f32[512,128]{1,0:T(8,128)S(1)}) custom-call(f32[1,4096,256]{2,1,0:T(8,128)} %tab.1, f32[32,128]{1,0:T(8,128)} %bitcast.2, s32[8]{0:T(128)} %slot_h.1, s32[8,2048]{1,0:T(8,128)} %ids_h.1, f32[1,16,2048]{2,1,0:T(8,128)} %grads.1), custom_call_target="tpu_custom_call" | custom-call | tf_op jit(solution)/shard_map/restore/pallas_call | solution.py:278
  59.7 2.2 %finish.1 = (f32[1,16,65536]{2,1,0:T(8,128)}, f32[512,128]{1,0:T(8,128)}) custom-call(f32[1,16,65536]{2,1,0:T(8,128)S(1)} %get-tuple-element.8.landed, f32[512,128]{1,0:T(8,128)S(1)} %get-tuple-element.9.state, f32[16,65536]{1,0:T(8,128)S(1)} %get-tuple-element.10.summed, f32[512,128]{1,0:T(8,128)S(1)} %get-tuple-element.11.rs), custom_call_target="tpu_custom_call" | custom-call | tf_op jit(solution)/shard_map/finish/pallas_call | solution.py:300

commit v5 on v3

--- a/solution.py
+++ b/solution.py
@@ -97,8 +97,8 @@
             cp.start()
             loads.append(cp)
 
-    def columns(h):
-        for i in range(CHUNKS):
+    def columns(h, chunks=range(CHUNKS)):
+        for i in chunks:
             loads[h * CHUNKS + i].wait()
             part = tabv[h, pl.ds(i * rows, rows), :]
             tT[h, :, :, pl.ds(i * rows, rows)] = part.T.reshape(8, 16, rows)
@@ -112,7 +112,7 @@
                 tT.at[1 - o[0], nz * 2 + nc], out.at[0, :, pl.ds(pl.multiple_of(col * BLK, BLK), BLK)],
                 (ssem, rsem), PEERS.index(o), (xl, y, lax.rem(xh + o[0], 2), nz, nc))
 
-    columns(0)
+    columns(0, range(CHUNKS // 2))
     for cp in small:
         cp.wait()
     pl.semaphore_wait(barrier, len(PEERS) + len(OTHERS))
@@ -121,6 +121,7 @@
     for i, o in enumerate(OTHERS):
         device, k = other(o)
         sends_a.append(remote(gv.at[:, pl.ds(pl.multiple_of(k * 256, 256), 256)], rA.at[src], (sA, rsA), i, device))
+    columns(0, range(CHUNKS // 2, CHUNKS))
     state_x = remote(stf.at[xh, z, c], stf.at[xh, z, c], (sst, rst), 0, peer((1, 0, 0)))
     send_tables(FIRST_X)
     columns(1)
@@ -198,15 +199,14 @@
         return 0
 
     q_core = remote(qs.at[1 - c], qp, (sq, rq_sem), 7, partner)
-    lax.fori_loop(0, 2, dense, 0)
+    lax.fori_loop(0, 1, dense, 0)
     q_core.wait()
     half = qs[c] + qp[...]
     qh[...] = half
     rq[xh * 4 + z] = half
-    lax.fori_loop(2, 3, dense, 0)
     sends_q = [remote(qh, rq.at[xh * 4 + z], (sq, rq_sem), i, peer((*o, 0))) for i, o in enumerate(CHIPS)]
     send_tables(THIRD)
-    lax.fori_loop(3, 14, dense, 0)
+    lax.fori_loop(1, 14, dense, 0)
     for cp in state_z:
         cp.wait_recv()
     state_c = remote(stf.at[:, :, c], stf.at[:, :, c], (sst, rst), 4, partner)

time: 62.2 us -> 62.2 us (level)
  no operation moved by 1% of the time
where the time goes in v5:
time: 62.2 us; the launch traced here: 61.6 us
  Pallas kernels  60.9 us (98%)
  between operations  0.64 us (1%)
    pallas_call x1, Pallas kernels, body(): pl.pallas_call(kernel, out_shape=(pltpu.VMEM((1, 16, ROWS), f32), pltpu.V...  58.7 us
    pallas_call x1, Pallas kernels, body(): pl.pallas_call(finish, out_shape=(jax.ShapeDtypeStruct((1, 16, ROWS), f32...  2.23 us

profile of v5, /device:TPU:1, one launch (start us, length us, event | category | flops | bytes accessed | tf_op | source)
XLA Modules:
  0.0 61.6 jit_solution(13592613234004651643)
XLA Ops:
  0.6 58.7 %restore.1 = (f32[1,16,65536]{2,1,0:T(8,128)S(1)}, f32[512,128]{1,0:T(8,128)S(1)}, f32[16,65536]{1,0:T(8,128)S(1)}, f32[512,128]{1,0:T(8,128)S(1)}) custom-call(f32[1,4096,256]{2,1,0:T(8,128)} %tab.1, f32[32,128]{1,0:T(8,128)} %bitcast.2, s32[8]{0:T(128)} %slot_h.1, s32[8,2048]{1,0:T(8,128)} %ids_h.1, f32[1,16,2048]{2,1,0:T(8,128)} %grads.1), custom_call_target="tpu_custom_call" | custom-call | tf_op jit(solution)/shard_map/restore/pallas_call | solution.py:278
  59.3 2.2 %finish.1 = (f32[1,16,65536]{2,1,0:T(8,128)}, f32[512,128]{1,0:T(8,128)}) custom-call(f32[1,16,65536]{2,1,0:T(8,128)S(1)} %get-tuple-element.8.landed, f32[512,128]{1,0:T(8,128)S(1)} %get-tuple-element.9.state, f32[16,65536]{1,0:T(8,128)S(1)} %get-tuple-element.10.summed, f32[512,128]{1,0:T(8,128)S(1)} %get-tuple-element.11.rs), custom_call_target="tpu_custom_call" | custom-call | tf_op jit(solution)/shard_map/finish/pallas_call | solution.py:300
